TPU v7x, 128 devices: a whole 4x4x4 slice. The times are simulated.
128 devices in a mesh: task: 8 (over x_hi, z), dp: 16 (over x_lo, y, core).
Axes of the slice: x: 4 (x_hi: 2, x_lo: 2; x = x_hi * 2 + x_lo), y: 4, z: 4, core: 2. Of those that a mesh axis runs over, the one named last changes fastest.
Arguments:
- tokens_in: bfloat16 [131072, 4096], P(('task', 'dp')), may hold values from -45 to 45
- query_cotangent: bfloat16 [131072, 2048], P(('task', 'dp')), may hold values from -23040 to 23040
- task_index: int32 [131072], P(('task', 'dp')), may hold values from 0 to 15, as said below
- loss_weights: int32 [16], replicated, may hold values from 1 to 4
- master: float32 [4096, 2048], P(('task', 'dp')), may hold values from -6 to 6
- moment_first: float32 [4096, 2048], P(('task', 'dp')), may hold values from -6 to 6
- moment_second: float32 [4096, 2048], P(('task', 'dp')), may hold values from 0.05 to 5
Outputs:
- new_master: float32 [4096, 2048], P(('task', 'dp'))
- new_first: float32 [4096, 2048], P(('task', 'dp'))
- new_second: float32 [4096, 2048], P(('task', 'dp'))
Inputs may be any that keep to these rules, and one draw needn't show every extreme that they name: `task_index`: the first 16 tokens name each task once.
All inputs are finite; a program needn't handle non-finite values.
Results may differ from a plain program's by a relative error of at most 0.00042.
Values may be sent and summed in bfloat16 or wider, within the bound.
A program may use at most 192 MiB of HBM per device.

v0:
```python
import jax
import jax.numpy as jnp
from jax import lax
from jax.sharding import Mesh
from jax.sharding import PartitionSpec as P

D = 4096
QW = 2048
TASK_DP = ("task_0", "task_1", "dp_0", "dp_1", "dp_2")
TASK = ("task_0", "task_1")
DP = ("dp_0", "dp_1", "dp_2")
beta_one = 0.9
beta_two = 0.95
adam_eps = 1e-08
step_rate = 0.01
decay_rate = 0.1
corr_one = 1.0 - 0.9**10
corr_two = 1.0 - 0.95**10


def over_axes(value, axes):
    for axis in axes:
        value = lax.psum(value, axis)
    return value


def split_up(value, dim, size):
    shape = value.shape
    blocks = value.reshape(*shape[:dim], size, shape[dim] // size, *shape[dim + 1 :])
    return jnp.moveaxis(blocks, dim, 0)


def summed_on_arrival(value, axis, dim):
    blocks = split_up(value, dim, lax.axis_size(axis))
    arrived = lax.all_to_all(blocks, axis, split_axis=0, concat_axis=0, tiled=True)
    return arrived.sum(axis=0)


def shards(
    tokens_in, query_cotangent, task_index, loss_weights, master, moment_first, moment_second
):
    labels = lax.iota(jnp.int32, loss_weights.shape[0])
    member = task_index[:, None] == labels[None, :]
    local_counts = jnp.sum(member.astype(jnp.int32), axis=0)
    counts = over_axes(local_counts, TASK_DP)
    task_scale = loss_weights.astype(jnp.float32) / counts.astype(jnp.float32)
    token_scale = jnp.sum(jnp.where(member, task_scale[None, :], jnp.float32(0.0)), axis=1)
    weighted = (query_cotangent.astype(jnp.float32) * token_scale[:, None]).astype(jnp.bfloat16)
    out_rows = master.shape[0]
    feature_count = weighted.shape[1]
    group_count = lax.axis_size(TASK)
    lane_count = lax.axis_size(DP)
    arranged = tokens_in.reshape(tokens_in.shape[0], group_count, lane_count, out_rows)
    group_rows = group_count * out_rows
    products = jnp.einsum("ntdr,nq->dtrq", arranged, weighted, preferred_element_type=jnp.float32)
    partial_value = lax.psum_scatter(
        products.reshape(lax.axis_size(DP) * group_rows, feature_count),
        DP,
        scatter_dimension=0,
        tiled=True,
    )
    gradient = summed_on_arrival(partial_value, TASK, 0)
    square_sum = over_axes(jnp.sum(gradient * gradient), TASK_DP)
    root_mean = jnp.sqrt(square_sum / (D * QW))
    factor = 1.0 / jnp.maximum(root_mean, 1.0)
    clipped = gradient * factor
    new_first = beta_one * moment_first + (1.0 - beta_one) * clipped
    new_second = beta_two * moment_second + (1.0 - beta_two) * clipped * clipped
    direction = new_first / corr_one / (jnp.sqrt(new_second / corr_two) + adam_eps)
    new_master = master - step_rate * (direction + decay_rate * master)
    return (new_master, new_first, new_second)


def solution(mesh):
    finer = Mesh(mesh.devices.reshape(2, 4, 2, 4, 2), ("task_0", "task_1", "dp_0", "dp_1", "dp_2"))
    in_specs = (
        P(TASK_DP, None),
        P(TASK_DP, None),
        P(TASK_DP),
        P(),
        P(TASK_DP, None),
        P(TASK_DP, None),
        P(TASK_DP, None),
    )
    out_specs = (P(TASK_DP, None), P(TASK_DP, None), P(TASK_DP, None))
    return jax.shard_map(
        shards, mesh=finer, in_specs=in_specs, out_specs=out_specs, check_vma=False
    )
```

profile of v0, /device:TPU:1, one launch (start us, length us, event | category | flops | bytes accessed | tf_op | source)
XLA Modules:
  0.0 349.0 jit_solution(1351179126321543253)
XLA Ops:
  7.2 0.0 reduce-scatter.2.cloned.1.call-start
  7.2 0.8 convert_reduce_fusion
  8.0 5.2 %psum.70 = s32[16]{0:T(128)S(1)} all-reduce(s32[16]{0:T(128)S(1)} %convert_reduce_fusion), channel_id=1, replica_groups=mesh['task_0'=2,'task_1'=4,'dp_0'=2,'dp_1'=4,'dp_2'=2] {'task_0'}, use_global_device_ids=true, to_apply=%region_1.0 | all-reduce | flops 16 | bytes 128 | tf_op jit(solution)/shard_map/psum | solution.py:23
  13.3 7.9 %psum.71 = s32[16]{0:T(128)S(1)} all-reduce(s32[16]{0:T(128)S(1)} %psum.70), channel_id=1, replica_groups=mesh['task_0'=2,'task_1'=4,'dp_0'=2,'dp_1'=4,'dp_2'=2] {'task_1'}, use_global_device_ids=true, to_apply=%region_2.0 | all-reduce | flops 16 | bytes 128 | tf_op jit(solution)/shard_map/psum | solution.py:23
  21.2 3.4 psum.72
  24.6 7.0 %psum.73 = s32[16]{0:T(128)S(1)} all-reduce(s32[16]{0:T(128)S(1)} %psum.72), channel_id=1, replica_groups=mesh['task_0'=2,'task_1'=4,'dp_0'=2,'dp_1'=4,'dp_2'=2] {'dp_1'}, use_global_device_ids=true, to_apply=%region_4.0 | all-reduce | flops 16 | bytes 128 | tf_op jit(solution)/shard_map/psum | solution.py:23
  31.6 8.2 %psum.74 = s32[16]{0:T(128)S(1)} all-reduce(s32[16]{0:T(128)S(1)} %psum.73), channel_id=1, replica_groups=mesh['task_0'=2,'task_1'=4,'dp_0'=2,'dp_1'=4,'dp_2'=2] {'dp_2'}, use_global_device_ids=true, to_apply=%region_5.0 | all-reduce | flops 16 | bytes 128 | tf_op jit(solution)/shard_map/psum | solution.py:23
  39.8 0.7 convert_divide_fusion
  40.4 0.8 select_reduce_fusion
  41.2 26.0 %fusion = f32[2048,4096]{0,1} fusion(bf16[1024,4096]{1,0:T(8,128)(2,1)} %param.7, bf16[1024,2048]{1,0:T(8,128)(2,1)} %param.8, f32[1024]{0:T(1024)S(1)} %select_reduce_fusion), kind=kOutput, calls=%fused_computation.1 | convolution fusion | flops 17186160640 | bytes 46141440
  67.2 23.0 %copy.14 = f32[16,8,32,2048]{3,2,1,0:T(8,128)} copy(f32[16,8,32,2048]{3,2,0,1:T(8,128)} %bitcast.10) | data formatting | bytes 67108864 | tf_op jit(solution)/shard_map/ntdr,nq->dtrq/transpose | solution.py:55
  90.2 0.0 copy-start
  90.2 0.0 copy-start.1
  90.2 0.0 copy-start.2
  90.2 0.0 reduce-scatter.2.cloned.1.call-update
  90.3 178.2 %reduce-scatter.2.cloned.1.call-done = f32[256,2048]{1,0:T(8,128)} async-done(((f32[4096,2048]{1,0:T(8,128)}), f32[256,2048]{1,0:T(8,128)}) %reduce-scatter.2.cloned.1.call-update) | async-done | bytes 2097168 | tf_op jit(solution)/shard_map/reduce_scatter | solution.py:56
  268.5 32.0 %all_to_all.5 = f32[8,32,2048]{2,1,0:T(8,128)S(1)} all-to-all(f32[8,32,2048]{2,1,0:T(8,128)} %bitcast.11), channel_id=1, replica_groups=mesh['task_0'=2,'task_1'=4,'dp_0'=2,'dp_1'=4,'dp_2'=2] {'task_0','task_1'}, dimensions={0} | all-to-all | bytes 4194304 | tf_op jit(solution)/shard_map/all_to_all | solution.py:35
  300.5 0.1 reduce_sum.38
  300.6 0.7 multiply_reduce_fusion
  301.2 5.9 %psum.75 = f32[]{:T(128)} all-reduce(f32[]{:T(128)} %multiply_reduce_fusion), channel_id=1, replica_groups=mesh['task_0'=2,'task_1'=4,'dp_0'=2,'dp_1'=4,'dp_2'=2] {'task_0'}, use_global_device_ids=true, to_apply=%region_10.11 | all-reduce | flops 1 | bytes 8 | tf_op jit(solution)/shard_map/psum | solution.py:23
  307.1 7.9 %psum.76 = f32[]{:T(128)} all-reduce(f32[]{:T(128)} %psum.75), channel_id=1, replica_groups=mesh['task_0'=2,'task_1'=4,'dp_0'=2,'dp_1'=4,'dp_2'=2] {'task_1'}, use_global_device_ids=true, to_apply=%region_11.12 | all-reduce | flops 1 | bytes 8 | tf_op jit(solution)/shard_map/psum | solution.py:23
  315.0 4.4 %psum.77 = f32[]{:T(128)} all-reduce(f32[]{:T(128)} %psum.76), channel_id=1, replica_groups=mesh['task_0'=2,'task_1'=4,'dp_0'=2,'dp_1'=4,'dp_2'=2] {'dp_0'}, use_global_device_ids=true, to_apply=%region_12.13 | all-reduce | flops 1 | bytes 8 | tf_op jit(solution)/shard_map/psum | solution.py:23
  319.4 11.5 %psum.78 = f32[]{:T(128)} all-reduce(f32[]{:T(128)} %psum.77), channel_id=1, replica_groups=mesh['task_0'=2,'task_1'=4,'dp_0'=2,'dp_1'=4,'dp_2'=2] {'dp_1'}, use_global_device_ids=true, to_apply=%region_13.14 | all-reduce | flops 1 | bytes 8 | tf_op jit(solution)/shard_map/psum | solution.py:23
  330.9 9.5 %psum.79 = f32[]{:T(128)} all-reduce(f32[]{:T(128)} %psum.78), channel_id=1, replica_groups=mesh['task_0'=2,'task_1'=4,'dp_0'=2,'dp_1'=4,'dp_2'=2] {'dp_2'}, use_global_device_ids=true, to_apply=%region_14.15 | all-reduce | flops 1 | bytes 8 | tf_op jit(solution)/shard_map/psum | solution.py:23
  341.1 0.0 copy-done
  341.2 0.0 copy-done.1
  341.2 0.0 copy-done.2
  341.2 1.0 multiply_subtract_fusion
Async XLA Ops:
  7.2 261.3 %reduce-scatter.2.cloned.1.call-start = ((), (), s32[]{:S(2)}) async-start(), calls=%async_computation.2 | async-start | bytes 35651584 | tf_op jit(solution)/shard_map/reduce_scatter | solution.py:56
  90.2 250.9 %copy-start = (f32[32,2048]{1,0:T(8,128)S(1)}, f32[32,2048]{1,0:T(8,128)}, u32[]{:S(2)}) copy-start(f32[32,2048]{1,0:T(8,128)} %param.11) | copy-start | bytes 786436
  90.2 250.9 %copy-start.1 = (f32[32,2048]{1,0:T(8,128)S(1)}, f32[32,2048]{1,0:T(8,128)}, u32[]{:S(2)}) copy-start(f32[32,2048]{1,0:T(8,128)} %param.12) | copy-start | bytes 786436
  90.2 250.9 %copy-start.2 = (f32[32,2048]{1,0:T(8,128)S(1)}, f32[32,2048]{1,0:T(8,128)}, u32[]{:S(2)}) copy-start(f32[32,2048]{1,0:T(8,128)} %param.13) | copy-start | bytes 786436
Sparse Core Ops, SparseCore 0:
  90.4 178.0 reduce-scatter.1
where the time goes:
time: 350 us; the launch traced here: 349 us
  waiting for transfers between devices  178 us (51%)
  blocking collectives  103 us (29%)
  matrix products  26 us (7%)
  local copies, waits for them, and re-layouts  23 us (7%)
  between operations  14.8 us (4%)
  other arithmetic  4.03 us (1%)
    reduce_scatter x1, waiting for transfers between devices, shards(): lax.psum_scatter(products.reshape(lax.axis_size(DP) * group_rows, feature...  178 us
    psum x10, blocking collectives, over_axes(): value = lax.psum(value, axis)  70.9 us
    all_to_all x1, blocking collectives, summed_on_arrival(): lax.all_to_all(blocks, axis, split_axis=0, concat_axis=0, tiled=True)  32 us
    unnamed x1, matrix products  26 us
    transpose x1, local copies, waits for them, and re-layouts, shards(): jnp.einsum('ntdr,nq->dtrq', arranged, weighted, preferred_element_type=jn...  23 us
  transfers between devices with their start and end apart: 1, of which 1 were waited for; matrix products, arithmetic and copies ran while one was open for 0% of the time, Pallas kernels for 0%

commit v1 on v0

--- a/solution.py
+++ b/solution.py
@@ -20,7 +20,7 @@
 
 def over_axes(value, axes):
     for axis in axes:
-        value = lax.psum(value, axis)
+        value = jnp.sum(lax.all_gather(value, axis_name=axis), axis=0)
     return value
 
 

time: 350 us -> 368 us (1.051)
  blocking collectives: 103 us -> 67.4 us
  waiting for transfers between devices: 178 us -> 204 us
  local copies, waits for them, and re-layouts: 23 us -> 38 us
  starting transfers between devices: 0.04 us -> 6.62 us
    psum x10 -> x0, blocking collectives: 70.9 us -> none  [over_axes(): value = lax.psum(value, axis)]
    unnamed x0 -> x10, blocking collectives: none -> 67.4 us
    all_to_all x1 -> x0, blocking collectives: 32 us -> none  [summed_on_arrival(): lax.all_to_all(blocks, axis, split_axis=0, concat_axis=0, tiled=True)]
    all_to_all x0 -> x1, waiting for transfers between devices: none -> 26.2 us  [summed_on_arrival(): lax.all_to_all(blocks, axis, split_axis=0, concat_axis=0, tiled=True)]
    unnamed x6 -> x31, local copies, waits for them, and re-layouts: 0.01 us -> 14.5 us
    all_to_all x0 -> x1, starting transfers between devices: none -> 6.58 us  [summed_on_arrival(): lax.all_to_all(blocks, axis, split_axis=0, concat_axis=0, tiled=True)]
  transfers between devices with their start and end apart: 1 -> 2, of which waited for: 1 -> 2; matrix products, arithmetic and copies ran while one was open for 0% -> 0% of each run, Pallas kernels for 0% -> 0%
where the time goes in v1:
time: 368 us
  waiting for transfers between devices  204 us (55%)
  blocking collectives  67.4 us (18%)
  local copies, waits for them, and re-layouts  38 us (10%)
  matrix products  26 us (7%)
  between operations  18.1 us (5%)
  other arithmetic  7.23 us (2%)
  starting transfers between devices  6.62 us (2%)
    reduce_scatter x1, waiting for transfers between devices, shards(): lax.psum_scatter(products.reshape(lax.axis_size(DP) * group_rows, feature...  178 us
    unnamed x10, blocking collectives  67.4 us
    all_to_all x1, waiting for transfers between devices, summed_on_arrival(): lax.all_to_all(blocks, axis, split_axis=0, concat_axis=0, tiled=True)  26.2 us
    unnamed x1, matrix products  26 us
    transpose x1, local copies, waits for them, and re-layouts, shards(): jnp.einsum('ntdr,nq->dtrq', arranged, weighted, preferred_element_type=jn...  23 us
    unnamed x31, local copies, waits for them, and re-layouts  14.5 us
  transfers between devices with their start and end apart: 2, of which 2 were waited for; matrix products, arithmetic and copies ran while one was open for 0% of the time, Pallas kernels for 0%

profile of v1, /device:TPU:1, one launch (start us, length us, event | category | flops | bytes accessed | tf_op | source)
XLA Modules:
  0.0 367.6 jit_solution(13079426077619168313)
XLA Ops:
  7.2 0.0 reduce-scatter.2.cloned.1.call-start
  7.2 0.8 convert_reduce_fusion
  8.0 1.2 dynamic-slice
  9.9 0.2 dynamic-update-slice
  10.2 5.2 %all-reduce = s32[32]{0:T(128)S(1)} all-reduce(s32[32]{0:T(128)S(1)} %dynamic-update-slice), channel_id=2, replica_groups=mesh['task_0'=2,'task_1'=4,'dp_0'=2,'dp_1'=4,'dp_2'=2] {'task_0'}, use_global_device_ids=true, to_apply=%add | all-reduce | flops 32 | bytes 256
  15.4 0.1 reshape.21
  15.5 1.2 dynamic-slice.1
  17.4 0.2 dynamic-update-slice.1
  17.6 7.9 %all-reduce.1 = s32[64]{0:T(128)S(1)} all-reduce(s32[64]{0:T(128)S(1)} %dynamic-update-slice.1), channel_id=3, replica_groups=mesh['task_0'=2,'task_1'=4,'dp_0'=2,'dp_1'=4,'dp_2'=2] {'task_1'}, use_global_device_ids=true, to_apply=%add.1 | all-reduce | flops 64 | bytes 512
  25.6 0.1 reshape.22
  25.6 1.2 dynamic-slice.2
  27.6 0.2 dynamic-update-slice.2
  27.8 3.1 all-reduce.2
  30.9 0.1 reshape.23
  31.0 1.2 dynamic-slice.3
  32.8 0.2 dynamic-update-slice.3
  33.1 7.0 %all-reduce.3 = s32[64]{0:T(128)S(1)} all-reduce(s32[64]{0:T(128)S(1)} %dynamic-update-slice.3), channel_id=5, replica_groups=mesh['task_0'=2,'task_1'=4,'dp_0'=2,'dp_1'=4,'dp_2'=2] {'dp_1'}, use_global_device_ids=true, to_apply=%add.3 | all-reduce | flops 64 | bytes 512
  40.1 0.1 reshape.24
  40.2 1.3 dynamic-slice.4
  42.2 0.2 dynamic-update-slice.4
  42.5 8.5 %all-reduce.4 = s32[32]{0:T(128)S(1)} all-reduce(s32[32]{0:T(128)S(1)} %dynamic-update-slice.4), channel_id=6, replica_groups=mesh['task_0'=2,'task_1'=4,'dp_0'=2,'dp_1'=4,'dp_2'=2] {'dp_2'}, use_global_device_ids=true, to_apply=%add.4 | all-reduce | flops 32 | bytes 256
  50.9 0.1 reshape.25
  51.0 0.7 convert_divide_fusion
  51.7 0.8 select_reduce_fusion
  52.5 26.0 %fusion = f32[2048,4096]{0,1} fusion(bf16[1024,4096]{1,0:T(8,128)(2,1)} %param.7, bf16[1024,2048]{1,0:T(8,128)(2,1)} %param.8, f32[1024]{0:T(1024)S(1)} %select_reduce_fusion), kind=kOutput, calls=%fused_computation.1 | convolution fusion | flops 17186160640 | bytes 46141440
  78.5 23.0 %copy.14 = f32[16,8,32,2048]{3,2,1,0:T(8,128)} copy(f32[16,8,32,2048]{3,2,0,1:T(8,128)} %bitcast.25) | data formatting | bytes 67108864 | tf_op jit(solution)/shard_map/ntdr,nq->dtrq/transpose | solution.py:55
  101.5 0.0 copy-start
  101.5 0.0 copy-start.1
  101.5 0.0 copy-start.2
  101.5 0.0 reduce-scatter.2.cloned.1.call-update
  101.5 178.2 %reduce-scatter.2.cloned.1.call-done = f32[256,2048]{1,0:T(8,128)} async-done(((f32[4096,2048]{1,0:T(8,128)}), f32[256,2048]{1,0:T(8,128)}) %reduce-scatter.2.cloned.1.call-update) | async-done | bytes 2097168 | tf_op jit(solution)/shard_map/reduce_scatter | solution.py:56
  279.7 6.6 %all-to-all-start = ((f32[8,32,2048]{2,1,0:T(8,128)}), f32[8,32,2048]{2,1,0:T(8,128)S(1)}, u32[]{:S(2)}, u32[]{:S(2)}) async-start(f32[8,32,2048]{2,1,0:T(8,128)} %bitcast.26), calls=%async_computation.1 | async-start | bytes 4194304 | tf_op jit(solution)/shard_map/all_to_all | solution.py:35
  286.3 26.2 %all-to-all-done = f32[8,32,2048]{2,1,0:T(8,128)S(1)} async-done(((f32[8,32,2048]{2,1,0:T(8,128)}), f32[8,32,2048]{2,1,0:T(8,128)S(1)}, u32[]{:S(2)}, u32[]{:S(2)}) %all-to-all-start) | async-done | bytes 2097184 | tf_op jit(solution)/shard_map/all_to_all | solution.py:35
  312.5 0.1 reduce_sum.133
  312.6 0.7 multiply_reduce_fusion
  313.3 1.4 dynamic-update-slice.5
  314.8 5.3 %all-reduce.5 = f32[2]{0:T(128)S(1)} all-reduce(f32[2]{0:T(128)S(1)} %dynamic-update-slice.5), channel_id=1, replica_groups=mesh['task_0'=2,'task_1'=4,'dp_0'=2,'dp_1'=4,'dp_2'=2] {'task_0'}, use_global_device_ids=true, to_apply=%add.5 | all-reduce | flops 2 | bytes 16
  320.0 0.6 reduce_sum.135
  320.7 1.4 dynamic-update-slice.6
  322.1 7.2 %all-reduce.6 = f32[4]{0:T(128)S(1)} all-reduce(f32[4]{0:T(128)S(1)} %dynamic-update-slice.6), channel_id=1, replica_groups=mesh['task_0'=2,'task_1'=4,'dp_0'=2,'dp_1'=4,'dp_2'=2] {'task_1'}, use_global_device_ids=true, to_apply=%add.6 | all-reduce | flops 4 | bytes 32
  329.2 0.6 reduce_sum.136
  329.8 1.4 dynamic-update-slice.7
  331.2 3.8 %all-reduce.7 = f32[2]{0:T(128)S(1)} all-reduce(f32[2]{0:T(128)S(1)} %dynamic-update-slice.7), channel_id=1, replica_groups=mesh['task_0'=2,'task_1'=4,'dp_0'=2,'dp_1'=4,'dp_2'=2] {'dp_0'}, use_global_device_ids=true, to_apply=%add.7 | all-reduce | flops 2 | bytes 16
  335.0 0.6 reduce_sum.137
  335.6 1.3 dynamic-update-slice.8
  336.9 10.6 %all-reduce.8 = f32[4]{0:T(128)S(1)} all-reduce(f32[4]{0:T(128)S(1)} %dynamic-update-slice.8), channel_id=1, replica_groups=mesh['task_0'=2,'task_1'=4,'dp_0'=2,'dp_1'=4,'dp_2'=2] {'dp_1'}, use_global_device_ids=true, to_apply=%add.8 | all-reduce | flops 4 | bytes 32
  347.5 0.6 reduce_sum.138
  348.1 1.4 dynamic-update-slice.9
  349.5 8.9 %all-reduce.9 = f32[2]{0:T(128)S(1)} all-reduce(f32[2]{0:T(128)S(1)} %dynamic-update-slice.9), channel_id=1, replica_groups=mesh['task_0'=2,'task_1'=4,'dp_0'=2,'dp_1'=4,'dp_2'=2] {'dp_2'}, use_global_device_ids=true, to_apply=%add.9 | all-reduce | flops 2 | bytes 16
  358.4 0.6 reduce_sum.139
  359.7 0.0 copy-done
  359.7 0.0 copy-done.1
  359.8 0.0 copy-done.2
  359.8 1.0 multiply_subtract_fusion
  (15 shorter events, 0.1 us)
Async XLA Ops:
  7.2 272.5 %reduce-scatter.2.cloned.1.call-start = ((), (), s32[]{:S(2)}) async-start(), calls=%async_computation.2 | async-start | bytes 35651584 | tf_op jit(solution)/shard_map/reduce_scatter | solution.py:56
  101.5 258.3 %copy-start = (f32[32,2048]{1,0:T(8,128)S(1)}, f32[32,2048]{1,0:T(8,128)}, u32[]{:S(2)}) copy-start(f32[32,2048]{1,0:T(8,128)} %param.11) | copy-start | bytes 786436
  101.5 258.3 %copy-start.1 = (f32[32,2048]{1,0:T(8,128)S(1)}, f32[32,2048]{1,0:T(8,128)}, u32[]{:S(2)}) copy-start(f32[32,2048]{1,0:T(8,128)} %param.12) | copy-start | bytes 786436
  101.5 258.3 %copy-start.2 = (f32[32,2048]{1,0:T(8,128)S(1)}, f32[32,2048]{1,0:T(8,128)}, u32[]{:S(2)}) copy-start(f32[32,2048]{1,0:T(8,128)} %param.13) | copy-start | bytes 786436
  279.7 32.8 %all-to-all-start = ((f32[8,32,2048]{2,1,0:T(8,128)}), f32[8,32,2048]{2,1,0:T(8,128)S(1)}, u32[]{:S(2)}, u32[]{:S(2)}) async-start(f32[8,32,2048]{2,1,0:T(8,128)} %bitcast.26), calls=%async_computation.1 | async-start | bytes 4194304 | tf_op jit(solution)/shard_map/all_to_all | solution.py:35
Sparse Core Ops, SparseCore 0:
  101.6 178.0 reduce-scatter.1
